TPU v7x, 32 devices: a whole 2x2x4 slice. The times are simulated.
32 devices in a mesh: seq: 16 (over z, x, core), head: 2 (over y).
Axes of the slice: x: 2, y: 2, z: 4, core: 2. Of those that a mesh axis runs over, the one named last changes fastest.
Arguments:
- hidden: bfloat16 [4608, 8192], P('seq'), may hold values from -6 to 6
- norm_gain: bfloat16 [8192], replicated, may hold values from 0.099609375 to 1.8984375
- w_query: bfloat16 [8192, 1024], P('seq', 'head'), may hold values from -0.125 to 0.125
- w_key: bfloat16 [8192, 256], P('seq', 'head'), may hold values from -0.125 to 0.125
- w_value: bfloat16 [8192, 256], P('seq', 'head'), may hold values from -0.0625 to 0.0625
- bias_query: bfloat16 [1024], P('head'), may hold values from -3 to 3
- bias_key: bfloat16 [256], P('head'), may hold values from -200 to 200
- bias_value: bfloat16 [256], P('head'), may hold values from -3 to 3
- w_out: bfloat16 [1024, 8192], P('head', 'seq'), may hold values from -0.1875 to 0.1875
Outputs:
- attn_out: bfloat16 [4608, 8192], P(('seq', 'head'))
All inputs are finite; a program needn't handle non-finite values.
Results may differ from a plain program's by a relative error of at most 0.014.
The roundings to bfloat16 on the way count: a program that leaves them out, or rounds other values in their place, can miss the bound.
Values may be sent and summed in bfloat16 or wider, within the bound.
No kernel may reach another device: no remote copies, remote signals or barrier semaphores. Data moves between devices by JAX's collectives and lax.ppermute only.
A program may use at most 192 MiB of HBM per device.

v0:
```python
import jax
import jax.numpy as jnp
from jax import lax
from jax.sharding import PartitionSpec as P

HEAD_DIM = 128
ROPE_BASE = 1000000.0
EPSILON = 1e-06


def rotary(values, positions):
    half_dim = values.shape[-1] // 2
    freq = ROPE_BASE ** (-2.0 * jnp.arange(half_dim, dtype=jnp.float32) / values.shape[-1])
    angles = positions.astype(jnp.float32)[:, None, None] * freq[None, None, :]
    cosine = jnp.cos(angles)
    sine = jnp.sin(angles)
    first = values[..., :half_dim]
    second = values[..., half_dim:]
    return jnp.concatenate(
        [first * cosine - second * sine, second * cosine + first * sine], axis=-1
    )


def local(hidden, norm_gain, w_query, w_key, w_value, bias_query, bias_key, bias_value, w_out):
    row_count = hidden.shape[0]
    head_count = w_query.shape[1] // HEAD_DIM
    first_row = lax.axis_index("seq") * row_count
    last_row = first_row + row_count - 1
    positions = first_row + jnp.arange(row_count, dtype=jnp.int32)
    widened = hidden.astype(jnp.float32)
    inverse = lax.rsqrt(jnp.mean(widened * widened, axis=-1, keepdims=True) + EPSILON)
    normed = (widened * inverse * norm_gain.astype(jnp.float32)).astype(jnp.bfloat16)
    query = jnp.dot(
        normed,
        lax.all_gather(w_query, "seq", axis=0, tiled=True),
        preferred_element_type=jnp.float32,
    )
    keys = jnp.dot(
        normed, lax.all_gather(w_key, "seq", axis=0, tiled=True), preferred_element_type=jnp.float32
    )
    values = jnp.dot(
        normed,
        lax.all_gather(w_value, "seq", axis=0, tiled=True),
        preferred_element_type=jnp.float32,
    )
    query = query + bias_query.astype(jnp.float32)
    keys = keys + bias_key.astype(jnp.float32)
    values = values + bias_value.astype(jnp.float32)
    query = rotary(query.reshape(row_count, head_count, HEAD_DIM), positions).astype(jnp.bfloat16)
    keys = (
        rotary(keys.reshape(row_count, 1, HEAD_DIM), positions)
        .reshape(row_count, HEAD_DIM)
        .astype(jnp.bfloat16)
    )
    values = values.astype(jnp.bfloat16)
    query_heads = query.transpose(1, 0, 2)
    scaling = HEAD_DIM ** (-0.5)
    initial = (
        jnp.full((head_count, row_count), -1e30, jnp.float32),
        jnp.zeros((head_count, row_count), jnp.float32),
        jnp.zeros((head_count, row_count, HEAD_DIM), jnp.float32),
    )
    key_piece = lax.all_gather(keys, "seq", axis=0, tiled=True)
    value_piece = lax.all_gather(values, "seq", axis=0, tiled=True)

    def update(state):
        highest, total, summed = state
        scores = (
            jnp.einsum("hqd,kd->hqk", query_heads, key_piece, preferred_element_type=jnp.float32)
            * scaling
        )
        key_positions = jnp.arange(key_piece.shape[0], dtype=jnp.int32)
        allowed = positions[:, None] >= key_positions[None, :]
        scores = jnp.where(allowed[None], scores, -jnp.inf)
        new_high = jnp.maximum(highest, jnp.max(scores, axis=-1))
        probs = jnp.exp(scores - new_high[..., None])
        total = jnp.sum(probs, axis=-1)
        mixed = jnp.einsum(
            "hqk,kd->hqd",
            probs.astype(jnp.bfloat16),
            value_piece,
            preferred_element_type=jnp.float32,
        )
        return (new_high, total, mixed)

    def unchanged(state):
        return state

    highest, total, summed = lax.cond(jnp.int32(0) <= last_row, update, unchanged, initial)
    attended = (summed / total[..., None]).astype(jnp.bfloat16)
    attended = attended.transpose(1, 0, 2).reshape(row_count, head_count * HEAD_DIM)
    partial_out = jnp.dot(
        attended,
        lax.all_gather(w_out, "seq", axis=1, tiled=True),
        preferred_element_type=jnp.float32,
    )
    result = lax.psum_scatter(
        partial_out.astype(jnp.bfloat16), "head", scatter_dimension=0, tiled=True
    )
    return result


def solution(mesh):
    in_specs = (
        P("seq", None),
        P(),
        P("seq", "head"),
        P("seq", "head"),
        P("seq", "head"),
        P("head"),
        P("head"),
        P("head"),
        P("head", "seq"),
    )
    out_specs = P(("seq", "head"), None)
    return jax.shard_map(local, mesh=mesh, in_specs=in_specs, out_specs=out_specs, check_vma=False)
```

profile of v0, /device:TPU:0, one launch (start us, length us, event | category | flops | bytes accessed | tf_op | source)
XLA Modules:
  0.0 401.3 jit_solution(17232137514900571910)
XLA Ops:
  6.5 0.7 all-gather.10.cloned.1.call-update
  7.3 0.7 all-gather.12.cloned.1.call-update
  8.1 0.7 all-gather.8.cloned.1.call-update
  8.8 0.7 convert_element_type.48
  9.5 0.7 convert_element_type.52
  10.2 3.4 fusion.11
  13.6 40.1 %all-gather.10.cloned.1.call-done = bf16[8192,128]{1,0:T(8,128)(2,1)} async-done(((bf16[512,128]{1,0:T(8,128)(2,1)}), bf16[8192,128]{1,0:T(8,128)(2,1)}) %all-gather.10.cloned.1.call-update) | async-done | bytes 2097168 | tf_op jit(solution)/shard_map/all_gather | solution.py:39
  53.7 4.6 %fusion.14 = f32[288,1,128]{2,0,1:T(8,128)S(1)} fusion(bf16[8192,128]{1,0:T(8,128)(2,1)} %all-gather.10.cloned.1.call-done, f32[128]{0:T(128)S(1)} %convert_element_type.52, bf16[288,8192]{1,0:T(8,128)(2,1)} %param.11, f32[8192]{0:T(1024)S(1)} %convert_element_type.48, f32[288]{0:T(512)S(1)} %add_rsqrt_fusion), kind=kOutput, calls=%fused_computation.24 | convolution fusion | flops 613453824 | bytes 6997632 | tf_op jit(solution)/shard_map/dot_general | solution.py:38
  58.3 0.7 fusion.24
  58.9 0.7 pad_maximum_fusion
  59.7 0.0 all-gather.14.cloned.1.call-start
  59.8 36.3 %all-gather.12.cloned.1.call-done = bf16[8192,128]{1,0:T(8,128)(2,1)} async-done(((bf16[512,128]{1,0:T(8,128)(2,1)}), bf16[8192,128]{1,0:T(8,128)(2,1)}) %all-gather.12.cloned.1.call-update) | async-done | bytes 2097168 | tf_op jit(solution)/shard_map/all_gather | solution.py:43
  96.1 5.1 %fusion.15 = bf16[288,128]{1,0:T(8,128)(2,1)} fusion(bf16[8192,128]{1,0:T(8,128)(2,1)} %all-gather.12.cloned.1.call-done, f32[128]{0:T(128)S(1)} %convert_element_type.54, bf16[288,8192]{1,0:T(8,128)(2,1)} %param.11, f32[8192]{0:T(1024)S(1)} %convert_element_type.48, f32[288]{0:T(512)S(1)} %add_rsqrt_fusion), kind=kOutput, calls=%fused_computation.25 | convolution fusion | flops 613490688 | bytes 6923904 | tf_op jit(solution)/shard_map/dot_general | solution.py:41
  101.3 0.5 all-gather.16.cloned.1.call-update
  101.8 0.2 reduce-scatter.2.cloned.1.call-start
  102.1 0.6 multiply_cosine_fusion.1
  102.7 68.6 %all-gather.8.cloned.1.call-done = bf16[8192,512]{1,0:T(8,128)(2,1)} async-done(((bf16[512,512]{1,0:T(8,128)(2,1)}), bf16[8192,512]{1,0:T(8,128)(2,1)}) %all-gather.8.cloned.1.call-update) | async-done | bytes 8388624 | tf_op jit(solution)/shard_map/all_gather | solution.py:35
  171.3 7.0 %convolution_add_fusion = f32[288,512]{1,0:T(8,128)S(1)} fusion(bf16[8192,512]{1,0:T(8,128)(2,1)} %all-gather.8.cloned.1.call-done, f32[512]{0:T(512)S(1)} %convert_element_type.50, bf16[288,8192]{1,0:T(8,128)(2,1)} %param.11, f32[8192]{0:T(1024)S(1)} %convert_element_type.48, f32[288]{0:T(512)S(1)} %add_rsqrt_fusion), kind=kOutput, calls=%fused_computation.21 | convolution fusion | flops 2425503744 | bytes 13732992 | tf_op jit(solution)/shard_map/dot_general | solution.py:33
  178.3 0.2 reshape.159
  178.6 0.4 fusion.30
  178.9 0.2 subtract_convert_fusion
  179.1 0.2 maximum_bitcast_fusion
  179.3 31.1 %all-gather.18.cloned.1.call-done = bf16[4608,1,128]{2,0,1:T(8,128)(2,1)} async-done(((bf16[288,1,128]{2,0,1:T(8,128)(2,1)}), bf16[4608,1,128]{2,0,1:T(8,128)(2,1)}) %all-gather.18.cloned.1.call-update) | async-done | bytes 1179664 | tf_op jit(solution)/shard_map/all_gather | solution.py:63
  210.3 39.3 %all-gather.14.cloned.1.call-done = bf16[4608,128]{1,0:T(8,128)(2,1)} async-done(((bf16[288,128]{1,0:T(8,128)(2,1)}), bf16[4608,128]{1,0:T(8,128)(2,1)}) %all-gather.14.cloned.1.call-update) | async-done | bytes 1179664 | tf_op jit(solution)/shard_map/all_gather | solution.py:64
  249.7 19.5 %conditional.1 = (f32[4,288]{1,0:T(4,128)S(1)}, f32[4,288,128]{2,1,0:T(8,128)S(1)}) conditional(s32[]{:T(128)} %convert_element_type.46, () %tuple.13, (s32[]{:T(128)}, s32[288]{0:T(512)S(1)}, bf16[4,288,128]{2,1,0:T(8,128)(2,1)S(1)}, bf16[4608,128]{1,0:T(8,128)(2,1)}, bf16[4608,128]{1,0:T(8,128)(2,1)}) %tuple.36), branch_computations={%region_1.0_spmd, %region_2.5_spmd} | conditional | flops 2777627648 | bytes 72284560 | solution.py:89
  249.7 0.8 iota_compare_fusion
  250.5 5.5 %fusion = (f32[4,288]{1,0:T(4,128)S(1)}, f32[4,288,4608]{2,1,0:T(8,128)S(1)}) fusion(pred[288,4608]{1,0:T(8,128)(4,1)S(1)} %iota_compare_fusion, bf16[4,288,128]{2,1,0:T(8,128)(2,1)S(1)} %get-tuple-element.19, bf16[4608,128]{1,0:T(8,128)(2,1)} %get-tuple-element.20), kind=kOutput, calls=%fused_computation.2 | convolution fusion | flops 1374878592 | bytes 24039936 | tf_op jit(solution)/shard_map/cond/branch_1_fun/hqd,kd->hqk/dot_general | solution.py:69
  255.9 6.6 %fusion.3 = f32[4,288,128]{2,1,0:T(8,128)S(1)} fusion(f32[4,288,4608]{2,1,0:T(8,128)S(1)} %get-tuple-element.27, f32[4,288]{1,0:T(4,128)S(1)} %broadcast_maximum_fusion, pred[288,4608]{1,0:T(8,128)(4,1)S(1)} %iota_compare_fusion, bf16[4608,128]{1,0:T(8,128)(2,1)} %get-tuple-element.21), kind=kOutput, calls=%fused_computation.5 | convolution fusion | flops 1380188160 | bytes 24334848 | tf_op jit(solution)/shard_map/cond/branch_1_fun/hqk,kd->hqd/dot_general | solution.py:78
  262.6 6.6 %fusion.2 = f32[4,288]{1,0:T(4,128)S(1)} fusion(f32[4,288,4608]{2,1,0:T(8,128)S(1)} %get-tuple-element.27, f32[4,288]{1,0:T(4,128)S(1)} %broadcast_maximum_fusion, pred[288,4608]{1,0:T(8,128)(4,1)S(1)} %iota_compare_fusion), kind=kLoop, calls=%fused_computation.4 | loop fusion | flops 21232512 | bytes 22569984 | tf_op jit(solution)/shard_map/cond/branch_1_fun/reduce_sum | solution.py:77
  269.2 59.2 %all-gather.16.cloned.1.call-done = bf16[512,8192]{1,0:T(8,128)(2,1)} async-done(((bf16[512,512]{1,0:T(8,128)(2,1)}), bf16[512,8192]{1,0:T(8,128)(2,1)}) %all-gather.16.cloned.1.call-update) | async-done | bytes 8388624 | tf_op jit(solution)/shard_map/all_gather | solution.py:94
  328.3 7.7 %convolution_convert_fusion = bf16[288,8192]{1,0:T(8,128)(2,1)} fusion(bf16[512,8192]{1,0:T(8,128)(2,1)} %all-gather.16.cloned.1.call-done, f32[4,288,128]{2,1,0:T(8,128)S(1)} %get-tuple-element.24, f32[4,288]{1,0:T(4,128)S(1)} %get-tuple-element.25), kind=kOutput, calls=%fused_computation.17 | convolution fusion | flops 2418573312 | bytes 13701632 | tf_op jit(solution)/shard_map/dot_general | solution.py:92
  336.1 58.4 %reduce-scatter.2.cloned.1.call-done = bf16[144,8192]{1,0:T(8,128)(2,1)} async-done(((bf16[288,8192]{1,0:T(8,128)(2,1)}), bf16[144,8192]{1,0:T(8,128)(2,1)}) %reduce-scatter.2.cloned.1.call-update) | async-done | bytes 2359312 | tf_op jit(solution)/shard_map/reduce_scatter | solution.py:97
  (20 shorter events, 0.3 us)
Async XLA Ops:
  6.5 47.2 %all-gather.10.cloned.1.call-start = ((), (), s32[]{:S(2)}) async-start(), calls=%async_computation.2 | async-start | bytes 2228224 | tf_op jit(solution)/shard_map/all_gather | solution.py:39
  7.3 88.8 %all-gather.12.cloned.1.call-start = ((), (), s32[]{:S(2)}) async-start(), calls=%async_computation.3 | async-start | bytes 2228224 | tf_op jit(solution)/shard_map/all_gather | solution.py:43
  8.0 163.3 %all-gather.8.cloned.1.call-start = ((), (), s32[]{:S(2)}) async-start(), calls=%async_computation.1 | async-start | bytes 8912896 | tf_op jit(solution)/shard_map/all_gather | solution.py:35
  8.7 201.6 %all-gather.18.cloned.1.call-start = ((), (), s32[]{:S(2)}) async-start(), calls=%async_computation.7 | async-start | bytes 1253376 | tf_op jit(solution)/shard_map/all_gather | solution.py:63
  13.5 46.2 %copy-start.1 = (bf16[128]{0:T(256)(128)(2,1)S(1)}, bf16[128]{0:T(256)(128)(2,1)}, u32[]{:S(2)}) copy-start(bf16[128]{0:T(256)(128)(2,1)} %param.18) | copy-start | bytes 772
  58.3 43.8 %copy-start = (bf16[512]{0:T(512)(128)(2,1)S(1)}, bf16[512]{0:T(512)(128)(2,1)}, u32[]{:S(2)}) copy-start(bf16[512]{0:T(512)(128)(2,1)} %param.16) | copy-start | bytes 3076
  59.7 190.0 %all-gather.14.cloned.1.call-start = ((), (), s32[]{:S(2)}) async-start(), calls=%async_computation.4 | async-start | bytes 1253376 | tf_op jit(solution)/shard_map/all_gather | solution.py:64
  101.2 227.1 %all-gather.16.cloned.1.call-start = ((), (), s32[]{:S(2)}) async-start(), calls=%async_computation.5 | async-start | bytes 8912896 | tf_op jit(solution)/shard_map/all_gather | solution.py:94
  101.8 292.6 %reduce-scatter.2.cloned.1.call-start = ((), (), s32[]{:S(2)}) async-start(), calls=%async_computation.6 | async-start | bytes 7077888 | tf_op jit(solution)/shard_map/reduce_scatter | solution.py:97
Sparse Core Ops, SparseCore 0:
  9.5 44.1 all-gather.9
  55.9 40.1 all-gather.11
  98.2 73.0 all-gather.7
  173.4 36.8 all-gather.17
  212.5 37.1 all-gather.13
  251.7 76.5 all-gather.15
  336.2 58.2 reduce-scatter.1
where the time goes:
time: 402 us; the launch traced here: 401 us
  waiting for transfers between devices  336 us (84%)
  matrix products  36.6 us (9%)
  other arithmetic  14.4 us (4%)
  between operations  13.6 us (3%)
    all_gather x1, waiting for transfers between devices, local(): lax.all_gather(w_query, 'seq', axis=0, tiled=True)  68.6 us
    all_gather x1, waiting for transfers between devices, local(): lax.all_gather(w_out, 'seq', axis=1, tiled=True)  59.2 us
    reduce_scatter x1, waiting for transfers between devices, local(): lax.psum_scatter(partial_out.astype(jnp.bfloat16), 'head', scatter_dimens...  58.4 us
    all_gather x1, waiting for transfers between devices, local(): lax.all_gather(w_key, 'seq', axis=0, tiled=True)  40.1 us
    all_gather x1, waiting for transfers between devices, local(): value_piece = lax.all_gather(values, 'seq', axis=0, tiled=True)  39.3 us
    all_gather x1, waiting for transfers between devices, local(): lax.all_gather(w_value, 'seq', axis=0, tiled=True)  36.3 us
    all_gather x1, waiting for transfers between devices, local(): key_piece = lax.all_gather(keys, 'seq', axis=0, tiled=True)  31.1 us
  transfers between devices with their start and end apart: 7, of which 7 were waited for; matrix products, arithmetic and copies ran while one was open for 11% of the time, Pallas kernels for 0%

commit v1 on v0

--- a/solution.py
+++ b/solution.py
@@ -6,6 +6,18 @@
 HEAD_DIM = 128
 ROPE_BASE = 1000000.0
 EPSILON = 1e-06
+
+
+def collect(array, axis, dim):
+    ways, here, step = (lax.axis_size(axis), lax.axis_index(axis), array.shape[dim])
+    line, have = (array, 1)
+    while have < ways:
+        line = jnp.concatenate(
+            [line, lax.ppermute(line, axis, [(d, (d - have) % ways) for d in range(ways)])],
+            axis=dim,
+        )
+        have = 2 * have
+    return jnp.roll(line, here * step, axis=dim)
 
 
 def rotary(values, positions):
@@ -61,7 +73,7 @@
         jnp.zeros((head_count, row_count, HEAD_DIM), jnp.float32),
     )
     key_piece = lax.all_gather(keys, "seq", axis=0, tiled=True)
-    value_piece = lax.all_gather(values, "seq", axis=0, tiled=True)
+    value_piece = collect(values, "seq", 0)
 
     def update(state):
         highest, total, summed = state

time: 402 us -> 390 us (0.970)
  waiting for transfers between devices: 336 us -> 311 us
  local copies, waits for them, and re-layouts: 0.59 us -> 7.01 us
    ppermute x0 -> x4, waiting for transfers between devices: none -> 85.4 us  [collect(): lax.ppermute(line, axis, [(d, (d - have) % ways) for d in range(ways)])]
    all_gather x1, waiting for transfers between devices: 68.6 us -> 1.76 us  [local(): lax.all_gather(w_query, 'seq', axis=0, tiled=True)]
    all_gather x1 -> x0, waiting for transfers between devices: 39.3 us -> none  [local(): value_piece = lax.all_gather(values, 'seq', axis=0, tiled=True)]
    unnamed x4 -> x12, local copies, waits for them, and re-layouts: 0.01 us -> 5.59 us
  transfers between devices with their start and end apart: 7 -> 10, of which waited for: 7 -> 10; matrix products, arithmetic and copies ran while one was open for 11% -> 13% of each run, Pallas kernels for 0% -> 0%
where the time goes in v1:
time: 390 us; the launch traced here: 389 us
  waiting for transfers between devices  311 us (80%)
  matrix products  38.8 us (10%)
  other arithmetic  15.2 us (4%)
  between operations  13.6 us (3%)
  local copies, waits for them, and re-layouts  7.01 us (2%)
  starting transfers between devices  3.9 us (1%)
    ppermute x4, waiting for transfers between devices, collect(): lax.ppermute(line, axis, [(d, (d - have) % ways) for d in range(ways)])  85.4 us
    reduce_scatter x1, waiting for transfers between devices, local(): lax.psum_scatter(partial_out.astype(jnp.bfloat16), 'head', scatter_dimens...  58.4 us
    all_gather x1, waiting for transfers between devices, local(): lax.all_gather(w_out, 'seq', axis=1, tiled=True)  57.8 us
    all_gather x1, waiting for transfers between devices, local(): lax.all_gather(w_key, 'seq', axis=0, tiled=True)  40.1 us
    all_gather x1, waiting for transfers between devices, local(): lax.all_gather(w_value, 'seq', axis=0, tiled=True)  35.7 us
    all_gather x1, waiting for transfers between devices, local(): key_piece = lax.all_gather(keys, 'seq', axis=0, tiled=True)  29 us
    dot_general x1, matrix products, local(): jnp.dot(attended, lax.all_gather(w_out, 'seq', axis=1, tiled=True), prefe...  8.48 us
    dot_general x1, matrix products, update(): jnp.einsum('hqk,kd->hqd', probs.astype(jnp.bfloat16), value_piece, prefer...  8.03 us
  transfers between devices with their start and end apart: 10, of which 10 were waited for; matrix products, arithmetic and copies ran while one was open for 13% of the time, Pallas kernels for 0%

profile of v1, /device:TPU:0, one launch (start us, length us, event | category | flops | bytes accessed | tf_op | source)
XLA Modules:
  0.0 389.3 jit_solution(499829141856792588)
XLA Ops:
  6.5 0.7 all-gather.9.cloned.1.call-update
  7.3 0.7 all-gather.11.cloned.1.call-update
  8.1 0.7 all-gather.7.cloned.1.call-update
  8.8 0.7 convert_element_type.51
  10.2 3.4 fusion.13
  13.6 40.1 %all-gather.9.cloned.1.call-done = bf16[8192,128]{1,0:T(8,128)(2,1)} async-done(((bf16[512,128]{1,0:T(8,128)(2,1)}), bf16[8192,128]{1,0:T(8,128)(2,1)}) %all-gather.9.cloned.1.call-update) | async-done | bytes 2097168 | tf_op jit(solution)/shard_map/all_gather | solution.py:51
  53.7 4.6 %fusion.16 = f32[288,1,128]{2,0,1:T(8,128)S(1)} fusion(bf16[8192,128]{1,0:T(8,128)(2,1)} %all-gather.9.cloned.1.call-done, f32[128]{0:T(128)S(1)} %convert_element_type.55, bf16[288,8192]{1,0:T(8,128)(2,1)} %param.11, f32[8192]{0:T(1024)S(1)} %convert_element_type.51, f32[288]{0:T(512)S(1)} %add_rsqrt_fusion), kind=kOutput, calls=%fused_computation.26 | convolution fusion | flops 613453824 | bytes 6997632 | tf_op jit(solution)/shard_map/dot_general | solution.py:50
  58.9 0.7 pad_maximum_fusion.3
  60.3 35.7 %all-gather.11.cloned.1.call-done = bf16[8192,128]{1,0:T(8,128)(2,1)} async-done(((bf16[512,128]{1,0:T(8,128)(2,1)}), bf16[8192,128]{1,0:T(8,128)(2,1)}) %all-gather.11.cloned.1.call-update) | async-done | bytes 2097168 | tf_op jit(solution)/shard_map/all_gather | solution.py:55
  96.1 5.2 %constant_dynamic-update-slice_fusion.9 = (bf16[9216,128]{1,0:T(8,128)(2,1)}, bf16[288,128]{1,0:T(8,128)(2,1)S(1)}) fusion(f32[128]{0:T(128)S(1)} %convert_element_type.57, bf16[8192,128]{1,0:T(8,128)(2,1)} %all-gather.11.cloned.1.call-done, bf16[288,8192]{1,0:T(8,128)(2,1)} %param.11, f32[8192]{0:T(1024)S(1)} %convert_element_type.51, ...), kind=kOutput, calls=%fused_computation.60 | convolution fusion | flops 613490688 | bytes 6997632 | tf_op jit(solution)/shard_map/dot_general | solution.py:53
  101.2 1.9 collective-permute-start
  103.1 2.0 collective-permute-done
  105.1 1.5 collective-permute-start.1
  106.6 7.9 %collective-permute-done.1 = bf16[576,128]{1,0:T(8,128)(2,1)S(1)} collective-permute-done((bf16[576,128]{1,0:T(8,128)(2,1)S(1)}, bf16[576,128]{1,0:T(8,128)(2,1)S(1)}, u32[]{:S(2)}, u32[]{:S(2)}) %collective-permute-start.1) | collective-permute-done | bytes 147488 | tf_op jit(solution)/shard_map/ppermute | solution.py:16
  114.8 19.5 %collective-permute-done.2 = bf16[1152,128]{1,0:T(8,128)(2,1)S(1)} collective-permute-done((bf16[1152,128]{1,0:T(8,128)(2,1)S(1)}, bf16[1152,128]{1,0:T(8,128)(2,1)S(1)}, u32[]{:S(2)}, u32[]{:S(2)}) %collective-permute-start.2) | collective-permute-done | bytes 294944 | tf_op jit(solution)/shard_map/ppermute | solution.py:16
  136.4 0.7 constant_dynamic-update-slice_fusion.6
  137.1 55.9 %collective-permute-done.3 = bf16[2304,128]{1,0:T(8,128)(2,1)S(1)} collective-permute-done((bf16[2304,128]{1,0:T(8,128)(2,1)S(1)}, bf16[2304,128]{1,0:T(8,128)(2,1)S(1)}, u32[]{:S(2)}, u32[]{:S(2)}) %collective-permute-start.3) | collective-permute-done | bytes 589856 | tf_op jit(solution)/shard_map/ppermute | solution.py:16
  193.0 0.9 constant_dynamic-update-slice_fusion.5
  195.8 0.7 constant_dynamic-update-slice_fusion.1
  196.6 0.9 constant_dynamic-update-slice_fusion
  197.4 1.8 all-gather.7.cloned.1.call-done
  199.2 7.0 %convolution_add_fusion = f32[288,512]{1,0:T(8,128)S(1)} fusion(bf16[8192,512]{1,0:T(8,128)(2,1)} %all-gather.7.cloned.1.call-done, f32[512]{0:T(512)S(1)} %convert_element_type.53, bf16[288,8192]{1,0:T(8,128)(2,1)} %param.11, f32[8192]{0:T(1024)S(1)} %convert_element_type.51, f32[288]{0:T(512)S(1)} %add_rsqrt_fusion), kind=kOutput, calls=%fused_computation.23 | convolution fusion | flops 2425503744 | bytes 13732992 | tf_op jit(solution)/shard_map/dot_general | solution.py:45
  207.0 0.9 maximum_bitcast_fusion
  207.9 29.0 %all-gather.15.cloned.1.call-done = bf16[4608,1,128]{2,0,1:T(8,128)(2,1)} async-done(((bf16[288,1,128]{2,0,1:T(8,128)(2,1)}), bf16[4608,1,128]{2,0,1:T(8,128)(2,1)}) %all-gather.15.cloned.1.call-update) | async-done | bytes 1179664 | tf_op jit(solution)/shard_map/all_gather | solution.py:75
  236.9 20.9 %conditional.1 = (f32[4,288]{1,0:T(4,128)S(1)}, f32[4,288,128]{2,1,0:T(8,128)}) conditional(s32[]{:T(128)} %convert_element_type.49, () %tuple.22, (s32[]{:T(128)}, s32[288]{0:T(512)S(1)}, bf16[4,288,128]{2,1,0:T(8,128)(2,1)}, bf16[4608,128]{1,0:T(8,128)(2,1)}, bf16[9216,128]{1,0:T(8,128)(2,1)}) %tuple.44), branch_computations={%region_1.2_spmd, %region_2.5_spmd} | conditional | flops 2777627648 | bytes 72284672 | solution.py:101
  236.9 0.8 iota_compare_fusion
  237.7 5.5 %fusion = (f32[4,288]{1,0:T(4,128)S(1)}, f32[4,288,4608]{2,1,0:T(8,128)S(1)}) fusion(pred[288,4608]{1,0:T(8,128)(4,1)S(1)} %iota_compare_fusion, bf16[4,288,128]{2,1,0:T(8,128)(2,1)} %get-tuple-element.106, bf16[4608,128]{1,0:T(8,128)(2,1)} %get-tuple-element.107), kind=kOutput, calls=%fused_computation.2 | convolution fusion | flops 1374878592 | bytes 24039936 | tf_op jit(solution)/shard_map/cond/branch_1_fun/hqd,kd->hqk/dot_general | solution.py:81
  243.2 8.0 %fusion.3 = f32[4,288,128]{2,1,0:T(8,128)} fusion(f32[4,288,4608]{2,1,0:T(8,128)S(1)} %get-tuple-element.114, f32[4,288]{1,0:T(4,128)S(1)} %broadcast_maximum_fusion, pred[288,4608]{1,0:T(8,128)(4,1)S(1)} %iota_compare_fusion, bf16[9216,128]{1,0:T(8,128)(2,1)} %get-tuple-element.108, s32[]{:T(128)S(6)} %select_n.26), kind=kOutput, calls=%fused_computation.5 | convolution fusion | flops 1380188160 | bytes 24334852 | tf_op jit(solution)/shard_map/cond/branch_1_fun/hqk,kd->hqd/dot_general | solution.py:90
  251.2 6.6 %fusion.2 = f32[4,288]{1,0:T(4,128)S(1)} fusion(f32[4,288,4608]{2,1,0:T(8,128)S(1)} %get-tuple-element.114, f32[4,288]{1,0:T(4,128)S(1)} %broadcast_maximum_fusion, pred[288,4608]{1,0:T(8,128)(4,1)S(1)} %iota_compare_fusion), kind=kLoop, calls=%fused_computation.4 | loop fusion | flops 21232512 | bytes 22569984 | tf_op jit(solution)/shard_map/cond/branch_1_fun/reduce_sum | solution.py:89
  257.8 57.8 %all-gather.13.cloned.1.call-done = bf16[512,8192]{1,0:T(8,128)(2,1)} async-done(((bf16[512,512]{1,0:T(8,128)(2,1)}), bf16[512,8192]{1,0:T(8,128)(2,1)}) %all-gather.13.cloned.1.call-update) | async-done | bytes 8388624 | tf_op jit(solution)/shard_map/all_gather | solution.py:106
  315.5 8.5 %convolution_convert_fusion = bf16[288,8192]{1,0:T(8,128)(2,1)} fusion(bf16[512,8192]{1,0:T(8,128)(2,1)} %all-gather.13.cloned.1.call-done, f32[4,288,128]{2,1,0:T(8,128)} %get-tuple-element.111, f32[4,288]{1,0:T(4,128)S(1)} %get-tuple-element.112), kind=kOutput, calls=%fused_computation.19 | convolution fusion | flops 2418573312 | bytes 13701632 | tf_op jit(solution)/shard_map/dot_general | solution.py:104
  324.0 58.4 %reduce-scatter.2.cloned.1.call-done = bf16[144,8192]{1,0:T(8,128)(2,1)} async-done(((bf16[288,8192]{1,0:T(8,128)(2,1)}), bf16[144,8192]{1,0:T(8,128)(2,1)}) %reduce-scatter.2.cloned.1.call-update) | async-done | bytes 2359312 | tf_op jit(solution)/shard_map/reduce_scatter | solution.py:109
  (37 shorter events, 7.1 us)
Async XLA Ops:
  6.5 47.2 %all-gather.9.cloned.1.call-start = ((), (), s32[]{:S(2)}) async-start(), calls=%async_computation.2 | async-start | bytes 2228224 | tf_op jit(solution)/shard_map/all_gather | solution.py:51
  7.3 88.8 %all-gather.11.cloned.1.call-start = ((), (), s32[]{:S(2)}) async-start(), calls=%async_computation.3 | async-start | bytes 2228224 | tf_op jit(solution)/shard_map/all_gather | solution.py:55
  8.0 191.2 %all-gather.7.cloned.1.call-start = ((), (), s32[]{:S(2)}) async-start(), calls=%async_computation.1 | async-start | bytes 8912896 | tf_op jit(solution)/shard_map/all_gather | solution.py:47
  8.7 228.2 %all-gather.15.cloned.1.call-start = ((), (), s32[]{:S(2)}) async-start(), calls=%async_computation.6 | async-start | bytes 1253376 | tf_op jit(solution)/shard_map/all_gather | solution.py:75
  13.6 46.8 %copy-start.1 = (bf16[128]{0:T(256)(128)(2,1)S(1)}, bf16[128]{0:T(256)(128)(2,1)}, u32[]{:S(2)}) copy-start(bf16[128]{0:T(256)(128)(2,1)} %param.18) | copy-start | bytes 772
  59.7 255.9 %all-gather.13.cloned.1.call-start = ((), (), s32[]{:S(2)}) async-start(), calls=%async_computation.4 | async-start | bytes 8912896 | tf_op jit(solution)/shard_map/all_gather | solution.py:106
  60.3 322.2 %reduce-scatter.2.cloned.1.call-start = ((), (), s32[]{:S(2)}) async-start(), calls=%async_computation.5 | async-start | bytes 7077888 | tf_op jit(solution)/shard_map/reduce_scatter | solution.py:109
  60.3 54.5 %copy-start = (bf16[512]{0:T(512)(128)(2,1)S(1)}, bf16[512]{0:T(512)(128)(2,1)}, u32[]{:S(2)}) copy-start(bf16[512]{0:T(512)(128)(2,1)} %param.16) | copy-start | bytes 3076
  101.2 3.9 collective-permute-start
  105.1 9.4 %collective-permute-start.1 = (bf16[576,128]{1,0:T(8,128)(2,1)S(1)}, bf16[576,128]{1,0:T(8,128)(2,1)S(1)}, u32[]{:S(2)}, u32[]{:S(2)}) collective-permute-start(bf16[576,128]{1,0:T(8,128)(2,1)S(1)} %pad_maximum_fusion.2), channel_id=1, source_target_pairs={{0,28},{2,30},{4,0},{6,2},{8,4},{10,6},{12,8},{14,10},{16,12},{18,... | collective-permute-start | bytes 442376 | tf_op jit(solution)/shard_map/ppermute | solution.py:16
  114.6 19.8 %collective-permute-start.2 = (bf16[1152,128]{1,0:T(8,128)(2,1)S(1)}, bf16[1152,128]{1,0:T(8,128)(2,1)S(1)}, u32[]{:S(2)}, u32[]{:S(2)}) collective-permute-start(bf16[1152,128]{1,0:T(8,128)(2,1)S(1)} %pad_maximum_fusion.1), channel_id=1, source_target_pairs={{0,24},{2,26},{4,28},{6,30},{8,0},{10,2},{12,4},{14,6},{16,8},{18,... | collective-permute-start | bytes 884744 | tf_op jit(solution)/shard_map/ppermute | solution.py:16
  134.4 58.7 %collective-permute-start.3 = (bf16[2304,128]{1,0:T(8,128)(2,1)S(1)}, bf16[2304,128]{1,0:T(8,128)(2,1)S(1)}, u32[]{:S(2)}, u32[]{:S(2)}) collective-permute-start(bf16[2304,128]{1,0:T(8,128)(2,1)S(1)} %pad_maximum_fusion), channel_id=1, source_target_pairs={{0,16},{2,18},{4,20},{6,22},{8,24},{10,26},{12,28},{14,30},{16,0},... | collective-permute-start | bytes 1769480 | tf_op jit(solution)/shard_map/ppermute | solution.py:16
Sparse Core Ops, SparseCore 0:
  9.5 44.1 all-gather.8
  55.9 40.1 all-gather.10
  98.2 100.9 all-gather.6
  201.3 35.5 all-gather.14
  238.9 76.5 all-gather.12
  324.2 58.2 reduce-scatter.1
